TPU v7x, 256 devices: a whole 4x4x8 slice. The times are simulated.
256 devices in a mesh: ep: 64 (over z, y, core), fsdp: 4 (over x).
Axes of the slice: x: 4, y: 4, z: 8, core: 2. Of those that a mesh axis runs over, the one named last changes fastest.
Arguments:
- train_gate: float32 [64, 2048, 1024], P('ep', 'fsdp'), may hold values from -0.1875 to 0.1875
- other_gate: bfloat16 [64, 2048, 1024], P('ep', 'fsdp'), may hold values from -0.0625 to 0.0625
- train_up: float32 [64, 2048, 1024], P('ep', 'fsdp'), may hold values from -0.1875 to 0.1875
- other_up: bfloat16 [64, 2048, 1024], P('ep', 'fsdp'), may hold values from -0.0625 to 0.0625
- router_weight: float32 [2048, 64], P('fsdp', 'ep'), may hold values from -0.125 to 0.125
- router_gain: float32 [2048], P('fsdp'), may hold values from 0.25 to 1.75
Outputs:
- ready_gate: bfloat16 [64, 2048, 1024], P('ep')
- ready_up: bfloat16 [64, 2048, 1024], P('ep')
- scale_gate: float32 [64, 1024], P('ep')
- scale_up: float32 [64, 1024], P('ep')
- serve_router: bfloat16 [2048, 64], replicated
All inputs are finite; a program needn't handle non-finite values.
Results may differ from a plain program's by a relative error of at most 0.001.
Values may be sent and summed in bfloat16 or wider, within the bound.
A program may use at most 64 MiB of HBM per device.

v0:
```python
import jax
import jax.numpy as jnp
from jax import lax
from jax.sharding import PartitionSpec as P


def copy_for_each(value, axis):
    copies = jnp.broadcast_to(value, (lax.axis_size(axis), *value.shape))
    return lax.all_to_all(copies, axis, split_axis=0, concat_axis=0, tiled=True)


def over_copies(value, axis):
    return copy_for_each(value, axis).sum(axis=0)


def packed_total(arrays, axis):
    flat, at, outs = (jnp.concatenate([a.reshape(-1) for a in arrays]), 0, [])
    so_far = over_copies(flat, axis)
    for a in arrays:
        outs.append(so_far[at : at + a.size].reshape(a.shape))
        at += a.size
    return tuple(outs)


def side_by_side(arrays, axis, dim, along):
    widths = [a.shape[along] for a in arrays]
    both = jnp.concatenate(arrays, axis=along)
    out = lax.all_gather(both, axis, axis=dim, tiled=True)
    return tuple(jnp.split(out, [sum(widths[:k]) for k in range(1, len(widths))], axis=along))


def joined_along(blocks, dim):
    dims = list(blocks.shape[1:])
    dims[dim] *= blocks.shape[0]
    return jnp.moveaxis(blocks, 0, dim).reshape(dims)


def gather_directly(value, axis, dim):
    return joined_along(copy_for_each(value, axis), dim)


def body(train_gate, other_gate, train_up, other_up, router_weight, router_gain):
    latest_gate = train_gate + other_gate.astype(jnp.float32)
    latest_up = train_up + other_up.astype(jnp.float32)
    total_gate, total_up = packed_total(
        (jnp.sum(latest_gate * latest_gate, axis=1), jnp.sum(latest_up * latest_up, axis=1)), "fsdp"
    )
    scale_gate = jnp.sqrt(total_gate)
    scale_up = jnp.sqrt(total_up)
    narrow_gate, narrow_up = (
        (latest_gate / jnp.expand_dims(scale_gate, 1)).astype(jnp.bfloat16),
        (latest_up / jnp.expand_dims(scale_up, 1)).astype(jnp.bfloat16),
    )
    ready_gate, ready_up = side_by_side((narrow_gate, narrow_up), "fsdp", 1, 0)
    part_router = (router_weight * router_gain[:, None]).astype(jnp.bfloat16)
    row_router = lax.all_gather(part_router, "fsdp", axis=0, tiled=True)
    serve_router = gather_directly(row_router, "ep", 1)
    return (ready_gate, ready_up, scale_gate, scale_up, serve_router)


def solution(mesh):
    placed = (
        P("ep", "fsdp", None),
        P("ep", "fsdp", None),
        P("ep", "fsdp", None),
        P("ep", "fsdp", None),
        P("fsdp", "ep"),
        P("fsdp"),
    )
    return jax.shard_map(
        body,
        mesh=mesh,
        in_specs=placed,
        out_specs=(P("ep", None, None), P("ep", None, None), P("ep", None), P("ep", None), P()),
        check_vma=False,
    )
```

profile of v0, /device:TPU:8, one launch (start us, length us, event | category | flops | bytes accessed | tf_op | source)
XLA Modules:
  0.0 124.0 jit_solution(4241068722860294294)
XLA Ops:
  7.2 0.0 all-gather.2.cloned.1.call-start
  7.2 3.6 %multiply_reduce_fusion = (f32[1024]{0:T(1024)S(1)}, f32[1024]{0:T(1024)S(1)}) fusion(f32[1,512,1024]{2,1,0:T(8,128)} %param.8, bf16[1,512,1024]{2,1,0:T(8,128)(2,1)} %param.9, f32[1,512,1024]{2,1,0:T(8,128)} %param.6, bf16[1,512,1024]{2,1,0:T(8,128)(2,1)} %param.7), kind=kLoop, calls=%fused_computation.3 | loop fusion | flops 4192256 | bytes 6299648 | tf_op jit(solution)/shard_map/reduce_sum | solution.py:46
  10.9 9.5 %all_to_all.11 = f32[4,1,2048]{2,1,0:T(1,128)S(1)} all-to-all(f32[4,1,2048]{2,1,0:T(1,128)S(1)} %broadcast_in_dim.11), channel_id=1, replica_groups=mesh['ep'=64,'fsdp'=4] {'fsdp'}, dimensions={0} | all-to-all | bytes 65536 | tf_op jit(solution)/shard_map/all_to_all | solution.py:9
  20.5 0.0 copy-start.4
  20.6 0.4 divide_convert_fusion
  21.0 0.1 copy-done.5
  21.1 0.0 copy-done.4
  21.1 1.0 copy-done.1
  22.1 0.3 copy-done.3
  22.4 0.4 divide_convert_fusion.1
  22.8 1.5 %pad_maximum_fusion = bf16[2,512,1024]{2,1,0:T(8,128)(2,1)} fusion(bf16[1,512,1024]{2,1,0:T(8,128)(2,1)S(1)} %divide_convert_fusion, bf16[1,512,1024]{2,1,0:T(8,128)(2,1)S(1)} %divide_convert_fusion.1), kind=kLoop, calls=%fused_computation | loop fusion | flops 1048576 | bytes 4194304 | tf_op jit(solution)/shard_map/concatenate | solution.py:27
  24.3 0.0 all-gather.2.cloned.1.call-update
  24.3 0.7 copy-done.6
  25.0 0.0 copy-done.7
  25.0 10.4 %all_gather.9 = bf16[2048,1]{0,1:T(2,128)(2,1)S(1)} all-gather(bf16[512,1]{0,1:T(2,128)(2,1)S(1)} %multiply_convert_fusion), channel_id=1, replica_groups=mesh['ep'=64,'fsdp'=4] {'fsdp'}, dimensions={0}, use_global_device_ids=true | all-gather | bytes 5120 | tf_op jit(solution)/shard_map/all_gather | solution.py:56
  35.5 0.3 broadcast_bitcast_fusion
  35.8 0.5 broadcast.9
  36.3 2.2 %reduce.4 = bf16[64,2048]{1,0:T(8,128)(2,1)S(1)} reduce(bf16[64,1,2048]{2,1,0:T(2,128)(2,1)S(1)} %broadcast_bitcast_fusion, bf16[]{:T(256)} %broadcast.9), dimensions={1}, to_apply=%broadcast_bitcast_fusion.reduce_sub_computation | reduce | bytes 524290
  38.4 0.2 reshape.38
  38.6 24.1 %all_to_all.12 = bf16[64,2,1024]{2,1,0:T(2,128)(2,1)S(1)} all-to-all(bf16[64,2,1024]{2,1,0:T(2,128)(2,1)S(1)} %reshape.38), channel_id=1, replica_groups=mesh['ep'=64,'fsdp'=4] {'ep'}, dimensions={0} | all-to-all | bytes 524288 | tf_op jit(solution)/shard_map/all_to_all | solution.py:9
  62.7 0.2 reshape.39
  62.9 0.9 copy.19
  63.8 47.3 %all-gather.2.cloned.1.call-done = bf16[2,2048,1024]{2,1,0:T(8,128)(2,1)} async-done(((bf16[2,512,1024]{2,1,0:T(8,128)(2,1)}), bf16[2,2048,1024]{2,1,0:T(8,128)(2,1)}) %all-gather.2.cloned.1.call-update) | async-done | bytes 8388624 | tf_op jit(solution)/shard_map/all_gather | solution.py:28
  111.1 6.0 %fusion = (bf16[1,2048,1024]{2,1,0:T(8,128)(2,1)}, bf16[1,2048,1024]{2,1,0:T(8,128)(2,1)}) fusion(bf16[2,2048,1024]{2,1,0:T(8,128)(2,1)} %all-gather.2.cloned.1.call-done), kind=kLoop, calls=%fused_computation.12 | loop fusion | bytes 16777216 | tf_op jit(solution)/shard_map/split | solution.py:29
  (15 shorter events, 0.1 us)
Async XLA Ops:
  7.2 13.4 %copy-start = (f32[1,512,1024]{2,1,0:T(8,128)S(1)}, f32[1,512,1024]{2,1,0:T(8,128)}, u32[]{:S(2)}) copy-start(f32[1,512,1024]{2,1,0:T(8,128)} %param.8) | copy-start | bytes 6291460
  7.2 13.4 %copy-start.2 = (bf16[1,512,1024]{2,1,0:T(8,128)(2,1)S(1)}, bf16[1,512,1024]{2,1,0:T(8,128)(2,1)}, u32[]{:S(2)}) copy-start(bf16[1,512,1024]{2,1,0:T(8,128)(2,1)} %param.9) | copy-start | bytes 3145732
  7.2 103.9 %all-gather.2.cloned.1.call-start = ((), (), s32[]{:S(2)}) async-start(), calls=%async_computation.2 | async-start | bytes 10485760 | tf_op jit(solution)/shard_map/all_gather | solution.py:28
  20.5 0.6 copy-start.5
  20.5 0.6 copy-start.4
  20.5 1.6 %copy-start.1 = (f32[1,512,1024]{2,1,0:T(8,128)S(1)}, f32[1,512,1024]{2,1,0:T(8,128)}, u32[]{:S(2)}) copy-start(f32[1,512,1024]{2,1,0:T(8,128)} %param.6) | copy-start | bytes 6291460
  20.6 1.8 %copy-start.3 = (bf16[1,512,1024]{2,1,0:T(8,128)(2,1)S(1)}, bf16[1,512,1024]{2,1,0:T(8,128)(2,1)}, u32[]{:S(2)}) copy-start(bf16[1,512,1024]{2,1,0:T(8,128)(2,1)} %param.7) | copy-start | bytes 3145732
  24.3 0.7 copy-start.6
  24.3 0.7 copy-start.7
Sparse Core Ops, SparseCore 0:
  24.5 86.6 all-gather.1
where the time goes:
time: 125 us; the launch traced here: 124 us
  waiting for transfers between devices  47.3 us (38%)
  blocking collectives  44.1 us (35%)
  between operations  14.2 us (11%)
  local copies, waits for them, and re-layouts  10.2 us (8%)
  other arithmetic  8.13 us (7%)
    all_gather x1, waiting for transfers between devices, side_by_side(): out = lax.all_gather(both, axis, axis=dim, tiled=True)  47.3 us
    all_to_all x2, blocking collectives, copy_for_each(): return lax.all_to_all(copies, axis, split_axis=0, concat_axis=0, tiled=True)  33.6 us
    all_gather x1, blocking collectives, body(): row_router = lax.all_gather(part_router, 'fsdp', axis=0, tiled=True)  10.4 us
    split x1, local copies, waits for them, and re-layouts, side_by_side(): jnp.split(out, [sum(widths[:k]) for k in range(1, len(widths))], axis=along)  6.02 us
    reduce_sum x1, other arithmetic, body(): jnp.sum(latest_up * latest_up, axis=1)  3.63 us
    unnamed x20, local copies, waits for them, and re-layouts  3.34 us
  transfers between devices with their start and end apart: 1, of which 1 were waited for; matrix products, arithmetic and copies ran while one was open for 3% of the time, Pallas kernels for 0%

commit v1 on v0

v1 whole, which is shorter than its diff:
```python
import functools

import jax
import jax.numpy as jnp
from jax import lax
from jax.experimental import pallas as pl
from jax.experimental.pallas import tpu as pltpu
from jax.sharding import PartitionSpec as P

MESH = pl.DeviceIdType.MESH
CHUNKS = 4
STEP = 16


def kernel(
    dims,
    tg_hbm, og_hbm, tu_hbm, ou_hbm, rw_ref, rg_ref,
    out_g, out_u, scale_g, scale_u, router,
    lat, oth, sums, rx, plane, zring,
    in_sem, sum_send, sum_recv, rx_send, rx_recv,
    own_send, own_recv, fwd_send, fwd_recv,
    pl_send, pl_recv, z_send, z_recv,
):
    nx, ny, nz, nc, rows = dims
    x = lax.axis_index("fsdp")
    e = lax.axis_index("ep")
    core = lax.rem(e, nc)
    y = lax.rem(lax.div(e, nc), ny)
    z = lax.div(e, nc * ny)

    def ep_of(zz, yy, cc):
        return (zz * ny + yy) * nc + cc

    def step(v, d, n):
        return lax.rem(v + d + n, n)

    right = (e, step(x, 1, nx))
    left = (e, step(x, -1, nx))
    across = (e, step(x, 2, nx))
    y_up = (ep_of(z, step(y, 1, ny), core), x)
    y_dn = (ep_of(z, step(y, -1, ny), core), x)
    z_up = (ep_of(step(z, 1, nz), y, core), x)
    z_dn = (ep_of(step(z, -1, nz), y, core), x)
    twin = (ep_of(z, y, step(core, 1, nc)), x)
    peers = (right, left, across, y_up, y_dn, z_up, z_dn, twin)

    barrier = pltpu.get_barrier_semaphore()
    for peer in peers:
        pl.semaphore_signal(barrier, inc=1, device_id=peer, device_id_type=MESH)

    size = rows // CHUNKS
    loads = []
    for t, (train, other) in enumerate(((tg_hbm, og_hbm), (tu_hbm, ou_hbm))):
        for c in range(CHUNKS):
            part = pl.ds(c * size, size)
            pair = (
                pltpu.make_async_copy(train.at[0, part], lat.at[t, part], in_sem.at[t, c, 0]),
                pltpu.make_async_copy(other.at[0, part], oth.at[t, part], in_sem.at[t, c, 1]),
            )
            for copy in pair:
                copy.start()
            loads.append(pair)

    def remote(src, dst, send, recv, peer):
        return pltpu.make_async_remote_copy(
            src_ref=src, dst_ref=dst, send_sem=send, recv_sem=recv,
            device_id=peer, device_id_type=MESH,
        )

    def local_sum(t):
        acc = jnp.zeros((8, lat.shape[2]), jnp.float32)
        for c in range(CHUNKS):
            for copy in loads[t * CHUNKS + c]:
                copy.wait()

            def add(i, acc, c=c):
                r = pl.multiple_of(c * size + i * STEP, STEP)
                v = lat[t, pl.ds(r, STEP), :] + oth[t, pl.ds(r, STEP), :].astype(jnp.float32)
                lat[t, pl.ds(r, STEP), :] = v
                v = v * v
                for k in range(STEP // 8):
                    acc = acc + v[8 * k : 8 * k + 8]
                return acc

            acc = lax.fori_loop(0, size // STEP, add, acc)
        return jnp.sum(acc, axis=0, keepdims=True)

    def spread(buf, send, recv):
        copies = []
        for k, peer in enumerate((right, left, across)):
            copy = remote(buf.at[x], buf.at[x], send.at[k], recv.at[k], peer)
            copy.start()
            copies.append(copy)
        return copies

    sums[0, x] = local_sum(0)
    pl.semaphore_wait(barrier, len(peers))
    pending = spread(sums.at[0], sum_send.at[0], sum_recv.at[0])
    rx[x] = rw_ref[...] * rg_ref[...]
    rx_copies = spread(rx, rx_send, rx_recv)
    sums[1, x] = local_sum(1)
    later = spread(sums.at[1], sum_send.at[1], sum_recv.at[1])

    outs, scales = (out_g, out_u), (scale_g, scale_u)
    own = []
    for t in range(2):
        for copy in (pending, later)[t]:
            copy.wait()
        total = sums[t, 0]
        for k in range(1, nx):
            total = total + sums[t, k]
        scale = jnp.sqrt(total)
        scales[t][...] = scale
        inv = jnp.broadcast_to(1.0 / scale, (STEP, lat.shape[2]))
        for c in range(CHUNKS):

            def narrow(i, carry, t=t, c=c, inv=inv):
                r = pl.multiple_of(c * size + i * STEP, STEP)
                w = pl.multiple_of(x * rows + c * size + i * STEP, STEP)
                outs[t][0, pl.ds(w, STEP), :] = (lat[t, pl.ds(r, STEP), :] * inv).astype(jnp.bfloat16)
                return carry

            lax.fori_loop(0, size // STEP, narrow, 0)
            where = pl.ds(pl.multiple_of(x * rows + c * size, size), size)
            piece = outs[t].at[0, where]
            for d, peer in enumerate((right, left)):
                copy = remote(piece, piece, own_send.at[d, t, c], own_recv.at[d, t, c], peer)
                copy.start()
                own.append(copy)

    for copy in rx_copies:
        copy.wait()
    mine = y * nc + core
    plane[mine] = jnp.concatenate([rx[k] for k in range(nx)], axis=1)
    first = remote(plane.at[mine], plane.at[mine], pl_send.at[0], pl_recv.at[0], twin)
    first.start()
    first.wait()
    near = pl.ds(y * nc, nc)
    ups = remote(plane.at[near], plane.at[near], pl_send.at[1], pl_recv.at[1], y_up)
    dns = remote(plane.at[near], plane.at[near], pl_send.at[2], pl_recv.at[2], y_dn)
    ups.start()
    dns.start()
    ups.wait()
    dns.wait()
    from_dn = pl.ds(step(y, -1, ny) * nc, nc)
    far = remote(plane.at[from_dn], plane.at[from_dn], pl_send.at[3], pl_recv.at[3], y_up)
    far.start()
    far.wait()
    zring[z] = jnp.concatenate([plane[k] for k in range(ny * nc)], axis=0)
    hops_up, hops_dn = nz // 2, nz - 1 - nz // 2
    for s in range(hops_up):
        at = step(z, -s, nz)
        moves = [remote(zring.at[at], zring.at[at], z_send.at[0, s], z_recv.at[0, s], z_up)]
        if s < hops_dn:
            at = step(z, s, nz)
            moves.append(remote(zring.at[at], zring.at[at], z_send.at[1, s], z_recv.at[1, s], z_dn))
        for copy in moves:
            copy.start()
        for copy in moves:
            copy.wait()
    for k in range(nz // 2):
        both = jnp.concatenate([zring[2 * k], zring[2 * k + 1]], axis=0)
        router[pl.ds(2 * k * ny * nc, 2 * ny * nc), :] = both.astype(jnp.bfloat16)

    fwd = []
    half = CHUNKS // 2
    for t in range(2):
        for c in range(CHUNKS):
            d = 0 if c < half else 1
            own[(t * CHUNKS + c) * 2 + d].wait_recv()
            source = step(x, -1, nx) if d == 0 else step(x, 1, nx)
            where = pl.ds(pl.multiple_of(source * rows + c * size, size), size)
            piece = outs[t].at[0, where]
            copy = remote(piece, piece, fwd_send.at[t, c], fwd_recv.at[t, c], (right, left)[d])
            copy.start()
            fwd.append(copy)
    for t in range(2):
        for c in range(CHUNKS):
            d = 0 if c < half else 1
            own[(t * CHUNKS + c) * 2 + 1 - d].wait_recv()
    for copy in own:
        copy.wait_send()
    for copy in fwd:
        copy.wait()


def body(dims, train_gate, other_gate, train_up, other_up, router_weight, router_gain):
    nx, ny, nz, nc, rows = dims
    width = train_gate.shape[2]
    whole = nx * rows
    experts = ny * nz * nc
    hbm = pl.BlockSpec(memory_space=pltpu.HBM)
    vmem = pl.BlockSpec(memory_space=pltpu.VMEM)
    dma = pltpu.SemaphoreType.DMA
    out = pl.pallas_call(
        functools.partial(kernel, dims),
        out_shape=(
            pltpu.VMEM((1, whole, width), jnp.bfloat16),
            pltpu.VMEM((1, whole, width), jnp.bfloat16),
            jax.ShapeDtypeStruct((1, width), jnp.float32),
            jax.ShapeDtypeStruct((1, width), jnp.float32),
            jax.ShapeDtypeStruct((experts, whole), jnp.bfloat16),
        ),
        in_specs=[hbm] * 4 + [vmem] * 2,
        out_specs=(vmem,) * 5,
        scratch_shapes=[
            pltpu.VMEM((2, rows, width), jnp.float32),
            pltpu.VMEM((2, rows, width), jnp.bfloat16),
            pltpu.VMEM((2, nx, 1, width), jnp.float32),
            pltpu.VMEM((nx, 1, rows), jnp.float32),
            pltpu.VMEM((ny * nc, 1, whole), jnp.float32),
            pltpu.VMEM((nz, ny * nc, whole), jnp.float32),
            dma((2, CHUNKS, 2)),
            dma((2, 3)), dma((2, 3)), dma((3,)), dma((3,)),
            dma((2, 2, CHUNKS)), dma((2, 2, CHUNKS)), dma((2, CHUNKS)), dma((2, CHUNKS)),
            dma((4,)), dma((4,)), dma((2, 4)), dma((2, 4)),
        ],
        compiler_params=pltpu.CompilerParams(
            collective_id=0, has_side_effects=True, vmem_limit_bytes=48 << 20
        ),
        name="ring",
    )(train_gate, other_gate, train_up, other_up, router_weight.T, router_gain[None, :])
    ready_gate, ready_up, scale_gate, scale_up, router = out
    return ready_gate, ready_up, scale_gate, scale_up, router.T


def solution(mesh):
    placed = (
        P("ep", "fsdp", None),
        P("ep", "fsdp", None),
        P("ep", "fsdp", None),
        P("ep", "fsdp", None),
        P("fsdp", "ep"),
        P("fsdp"),
    )
    nx, ep = mesh.shape["fsdp"], mesh.shape["ep"]
    dims = (nx, 4, ep // 8, 2, 2048 // nx)
    return jax.shard_map(
        functools.partial(body, dims),
        mesh=mesh,
        in_specs=placed,
        out_specs=(P("ep", None, None), P("ep", None, None), P("ep", None), P("ep", None), P()),
        check_vma=False,
    )
```

time: 125 us -> 87.9 us (0.70)
  Pallas kernels: 0 us -> 81.2 us
  waiting for transfers between devices: 47.3 us -> 0 us
  blocking collectives: 44.1 us -> 0 us
  between operations: 14.2 us -> 0.65 us
  other arithmetic: 8.13 us -> 0 us
  local copies, waits for them, and re-layouts: 10.2 us -> 5.93 us
    pallas_call x0 -> x1, Pallas kernels: none -> 81.2 us  [body(): pl.pallas_call(functools.partial(kernel, dims), out_shape=(pltpu.VMEM((1,...]
    all_gather x1 -> x0, waiting for transfers between devices: 47.3 us -> none  [side_by_side(): out = lax.all_gather(both, axis, axis=dim, tiled=True)]
    all_to_all x2 -> x0, blocking collectives: 33.6 us -> none  [copy_for_each(): return lax.all_to_all(copies, axis, split_axis=0, concat_axis=0, tiled=True)]
    all_gather x1 -> x0, blocking collectives: 10.4 us -> none  [body(): row_router = lax.all_gather(part_router, 'fsdp', axis=0, tiled=True)]
    split x1 -> x0, local copies, waits for them, and re-layouts: 6.02 us -> none  [side_by_side(): jnp.split(out, [sum(widths[:k]) for k in range(1, len(widths))], axis=along)]
    reduce_sum x2 -> x0, other arithmetic: 3.66 us -> none  [the longest x1 3.63 us: body(): jnp.sum(latest_up * latest_up, axis=1)]
    unnamed x20 -> x11, local copies, waits for them, and re-layouts: 3.34 us -> 5.93 us
    unnamed x1 -> x0, other arithmetic: 2.16 us -> none
  transfers between devices with their start and end apart: 1 -> 0, of which waited for: 1 -> 0; matrix products, arithmetic and copies ran while one was open for 3% -> 0% of each run, Pallas kernels for 0% -> 0%
where the time goes in v1:
time: 87.9 us; the launch traced here: 87.7 us
  Pallas kernels  81.2 us (92%)
  local copies, waits for them, and re-layouts  5.93 us (7%)
    pallas_call x1, Pallas kernels, body(): pl.pallas_call(functools.partial(kernel, dims), out_shape=(pltpu.VMEM((1,...  81.2 us
    unnamed x11, local copies, waits for them, and re-layouts  5.93 us

profile of v1, /device:TPU:8, one launch (start us, length us, event | category | flops | bytes accessed | tf_op | source)
XLA Modules:
  0.0 87.7 jit_solution(7983597119444962436)
XLA Ops:
  0.6 81.2 %ring.1 = (bf16[1,2048,1024]{2,1,0:T(8,128)(2,1)S(1)}, bf16[1,2048,1024]{2,1,0:T(8,128)(2,1)S(1)}, f32[1,1024]{1,0:T(1,128)}, f32[1,1024]{1,0:T(1,128)}, bf16[64,2048]{1,0:T(8,128)(2,1)}) custom-call(f32[1,512,1024]{2,1,0:T(8,128)} %tg_hbm.1, bf16[1,512,1024]{2,1,0:T(8,128)(2,1)} %og_hbm.1, f32[1,512,1024]{2,1,0:T(8,128)} %tu_hbm.1, ...), custom_call_target="tpu_custom_call" | custom-call | tf_op jit(solution)/shard_map/ring/pallas_call | solution.py:195
  81.8 2.0 %copy.16 = bf16[1,2048,1024]{2,1,0:T(8,128)(2,1)} copy(bf16[1,2048,1024]{2,1,0:T(8,128)(2,1)S(1)} %get-tuple-element.15) | data formatting | bytes 8388608
  83.8 0.0 copy-start.2
  83.8 0.0 copy-start.1
  83.8 0.0 copy-start
  83.8 2.0 %copy.17 = bf16[1,2048,1024]{2,1,0:T(8,128)(2,1)} copy(bf16[1,2048,1024]{2,1,0:T(8,128)(2,1)S(1)} %get-tuple-element.16) | data formatting | bytes 8388608
  85.8 0.0 copy-done.2
  85.8 0.6 copy.18
  86.4 0.0 copy-done.1
  86.4 0.6 copy.19
  87.0 0.0 copy-done
  87.0 0.7 copy.20
Async XLA Ops:
  83.8 2.0 %copy-start.2 = (f32[1,1024]{1,0:T(1,128)S(1)}, f32[1,1024]{1,0:T(1,128)}, u32[]{:S(2)}) copy-start(f32[1,1024]{1,0:T(1,128)} %get-tuple-element.27) | copy-start | bytes 12292
  83.8 2.6 %copy-start.1 = (f32[1,1024]{1,0:T(1,128)S(1)}, f32[1,1024]{1,0:T(1,128)}, u32[]{:S(2)}) copy-start(f32[1,1024]{1,0:T(1,128)} %get-tuple-element.28) | copy-start | bytes 12292
  83.8 3.2 %copy-start = (bf16[64,2048]{1,0:T(8,128)(2,1)S(1)}, bf16[64,2048]{1,0:T(8,128)(2,1)}, u32[]{:S(2)}) copy-start(bf16[64,2048]{1,0:T(8,128)(2,1)} %get-tuple-element.14) | copy-start | bytes 786436

commit v2 on v1

--- a/solution.py
+++ b/solution.py
@@ -10,6 +10,7 @@
 MESH = pl.DeviceIdType.MESH
 CHUNKS = 4
 STEP = 16
+PARTS = 4
 
 
 def kernel(
@@ -42,11 +43,17 @@
     z_up = (ep_of(step(z, 1, nz), y, core), x)
     z_dn = (ep_of(step(z, -1, nz), y, core), x)
     twin = (ep_of(z, y, step(core, 1, nc)), x)
-    peers = (right, left, across, y_up, y_dn, z_up, z_dn, twin)
+    row = (right, left, across)
+    grid = (y_up, y_dn, z_up, z_dn)
 
     barrier = pltpu.get_barrier_semaphore()
-    for peer in peers:
-        pl.semaphore_signal(barrier, inc=1, device_id=peer, device_id_type=MESH)
+    odd = lax.rem(y + z, 2)
+
+    def greet(them):
+        for peer in them:
+            pl.semaphore_signal(barrier, inc=1, device_id=peer, device_id_type=MESH)
+
+    greet(row)
 
     size = rows // CHUNKS
     loads = []
@@ -94,7 +101,8 @@
         return copies
 
     sums[0, x] = local_sum(0)
-    pl.semaphore_wait(barrier, len(peers))
+    pl.semaphore_wait(barrier, len(row) + len(grid) * odd + core)
+    greet(grid + (twin,))
     pending = spread(sums.at[0], sum_send.at[0], sum_recv.at[0])
     rx[x] = rw_ref[...] * rg_ref[...]
     rx_copies = spread(rx, rx_send, rx_recv)
@@ -127,6 +135,12 @@
                 copy = remote(piece, piece, own_send.at[d, t, c], own_recv.at[d, t, c], peer)
                 copy.start()
                 own.append(copy)
+
+    answers = len(grid) * (1 - odd) + (1 - core)
+
+    @pl.when(answers > 0)
+    def _():
+        pl.semaphore_wait(barrier, answers)
 
     for copy in rx_copies:
         copy.wait()
@@ -184,6 +198,22 @@
         copy.wait()
 
 
+def write_out(*refs):
+    held, outs, sem = refs[:5], refs[5:10], refs[10]
+    copies = []
+    for k in range(2):
+        size = held[k].shape[1] // PARTS
+        for p in range(PARTS):
+            part = (0, pl.ds(p * size, size))
+            copies.append(pltpu.make_async_copy(held[k].at[part], outs[k].at[part], sem.at[k, p]))
+    for k in range(2, 5):
+        copies.append(pltpu.make_async_copy(held[k], outs[k], sem.at[k, 0]))
+    for copy in copies:
+        copy.start()
+    for copy in copies:
+        copy.wait()
+
+
 def body(dims, train_gate, other_gate, train_up, other_up, router_weight, router_gain):
     nx, ny, nz, nc, rows = dims
     width = train_gate.shape[2]
@@ -197,9 +227,9 @@
         out_shape=(
             pltpu.VMEM((1, whole, width), jnp.bfloat16),
             pltpu.VMEM((1, whole, width), jnp.bfloat16),
-            jax.ShapeDtypeStruct((1, width), jnp.float32),
-            jax.ShapeDtypeStruct((1, width), jnp.float32),
-            jax.ShapeDtypeStruct((experts, whole), jnp.bfloat16),
+            pltpu.VMEM((1, width), jnp.float32),
+            pltpu.VMEM((1, width), jnp.float32),
+            pltpu.VMEM((experts, whole), jnp.bfloat16),
         ),
         in_specs=[hbm] * 4 + [vmem] * 2,
         out_specs=(vmem,) * 5,
@@ -220,7 +250,15 @@
         ),
         name="ring",
     )(train_gate, other_gate, train_up, other_up, router_weight.T, router_gain[None, :])
-    ready_gate, ready_up, scale_gate, scale_up, router = out
+    ready_gate, ready_up, scale_gate, scale_up, router = pl.pallas_call(
+        write_out,
+        out_shape=tuple(jax.ShapeDtypeStruct(o.shape, o.dtype) for o in out),
+        in_specs=[vmem] * 5,
+        out_specs=(hbm,) * 5,
+        scratch_shapes=[dma((5, PARTS))],
+        compiler_params=pltpu.CompilerParams(vmem_limit_bytes=4 << 20),
+        name="write_out",
+    )(*out)
     return ready_gate, ready_up, scale_gate, scale_up, router.T
 
 

time: 87.9 us -> 88.1 us (level)
  Pallas kernels: 81.2 us -> 87.3 us
  local copies, waits for them, and re-layouts: 5.93 us -> 0 us
    unnamed x11 -> x0, local copies, waits for them, and re-layouts: 5.93 us -> none
    pallas_call x0 -> x1, Pallas kernels: none -> 3.53 us  [body(): pl.pallas_call(write_out, out_shape=tuple((jax.ShapeDtypeStruct(o.shape,...]
    pallas_call x1, Pallas kernels: 81.2 us -> 83.8 us  [body(): pl.pallas_call(functools.partial(kernel, dims), out_shape=(pltpu.VMEM((1,...]
where the time goes in v2:
time: 88.1 us; the launch traced here: 87.9 us
  Pallas kernels  87.3 us (99%)
    pallas_call x1, Pallas kernels, body(): pl.pallas_call(functools.partial(kernel, dims), out_shape=(pltpu.VMEM((1,...  83.8 us
    pallas_call x1, Pallas kernels, body(): pl.pallas_call(write_out, out_shape=tuple((jax.ShapeDtypeStruct(o.shape,...  3.53 us

profile of v2, /device:TPU:8, one launch (start us, length us, event | category | flops | bytes accessed | tf_op | source)
XLA Modules:
  0.0 87.9 jit_solution(18368196150837179690)
XLA Ops:
  0.6 83.8 %ring.1 = (bf16[1,2048,1024]{2,1,0:T(8,128)(2,1)S(1)}, bf16[1,2048,1024]{2,1,0:T(8,128)(2,1)S(1)}, f32[1,1024]{1,0:T(1,128)S(1)}, f32[1,1024]{1,0:T(1,128)S(1)}, bf16[64,2048]{1,0:T(8,128)(2,1)S(1)}) custom-call(f32[1,512,1024]{2,1,0:T(8,128)} %tg_hbm.1, bf16[1,512,1024]{2,1,0:T(8,128)(2,1)} %og_hbm.1, f32[1,512,1024]{2,1,0:T(8,128)} %tu_hbm.1, ...), custom_call_target="tpu_custom_call" | custom-call | tf_op jit(solution)/shard_map/ring/pallas_call | solution.py:225
  84.4 3.5 %write_out.1 = (bf16[1,2048,1024]{2,1,0:T(8,128)(2,1)}, bf16[1,2048,1024]{2,1,0:T(8,128)(2,1)}, f32[1,1024]{1,0:T(1,128)}, f32[1,1024]{1,0:T(1,128)}, bf16[64,2048]{1,0:T(8,128)(2,1)}) custom-call(bf16[1,2048,1024]{2,1,0:T(8,128)(2,1)S(1)} %get-tuple-element.15.refs_0_, bf16[1,2048,1024]{2,1,0:T(8,128)(2,1)S(1)} %get-tuple-element.16.refs_1_, ...), custom_call_target="tpu_custom_call" | custom-call | tf_op jit(solution)/shard_map/write_out/pallas_call | solution.py:253

commit v3 on v2

--- a/solution.py
+++ b/solution.py
@@ -11,29 +11,39 @@
 CHUNKS = 4
 STEP = 16
 PARTS = 4
+RAW = 64
+SPLIT = 2
 
 
 def kernel(
     dims,
     tg_hbm, og_hbm, tu_hbm, ou_hbm, rw_ref, rg_ref,
     out_g, out_u, scale_g, scale_u, router,
-    lat, oth, sums, rx, plane, zring,
-    in_sem, sum_send, sum_recv, rx_send, rx_recv,
+    lat, oth, sums, raw, rx, plane, zring,
+    in_sem, sum_send, sum_recv, raw_send, raw_recv, rx_send, rx_recv,
     own_send, own_recv, fwd_send, fwd_recv,
-    pl_send, pl_recv, z_send, z_recv,
+    pl_send, pl_recv, z_send, z_recv, answer_sem,
 ):
     nx, ny, nz, nc, rows = dims
+    width = lat.shape[2]
     x = lax.axis_index("fsdp")
     e = lax.axis_index("ep")
     core = lax.rem(e, nc)
     y = lax.rem(lax.div(e, nc), ny)
     z = lax.div(e, nc * ny)
+    y_odd, z_odd = lax.rem(y, 2), lax.rem(z, 2)
 
     def ep_of(zz, yy, cc):
         return (zz * ny + yy) * nc + cc
 
     def step(v, d, n):
         return lax.rem(v + d + n, n)
+
+    def remote(src, dst, send, recv, peer):
+        return pltpu.make_async_remote_copy(
+            src_ref=src, dst_ref=dst, send_sem=send, recv_sem=recv,
+            device_id=peer, device_id_type=MESH,
+        )
 
     right = (e, step(x, 1, nx))
     left = (e, step(x, -1, nx))
@@ -43,104 +53,142 @@
     z_up = (ep_of(step(z, 1, nz), y, core), x)
     z_dn = (ep_of(step(z, -1, nz), y, core), x)
     twin = (ep_of(z, y, step(core, 1, nc)), x)
-    row = (right, left, across)
-    grid = (y_up, y_dn, z_up, z_dn)
 
     barrier = pltpu.get_barrier_semaphore()
-    odd = lax.rem(y + z, 2)
-
-    def greet(them):
-        for peer in them:
-            pl.semaphore_signal(barrier, inc=1, device_id=peer, device_id_type=MESH)
-
-    greet(row)
-
+    for peer in (right, left, across):
+        pl.semaphore_signal(barrier, inc=1, device_id=peer, device_id_type=MESH)
+    pairs = ((z_odd, (z_up, z_dn)), (y_odd, (y_up, y_dn)), (core, (twin,)))
+    for side, them in pairs:
+
+        @pl.when(side == 0)
+        def _(them=them):
+            for peer in them:
+                pl.semaphore_signal(barrier, inc=1, device_id=peer, device_id_type=MESH)
+
+    part = width // SPLIT
+    items = [(0, k * part, part) for k in range(SPLIT)] + [(1, 0, width)]
     size = rows // CHUNKS
     loads = []
-    for t, (train, other) in enumerate(((tg_hbm, og_hbm), (tu_hbm, ou_hbm))):
-        for c in range(CHUNKS):
-            part = pl.ds(c * size, size)
+    for i, (t, col, wide) in enumerate(items):
+        train, other = ((tg_hbm, og_hbm), (tu_hbm, ou_hbm))[t]
+        for c in range(CHUNKS):
+            at = (pl.ds(c * size, size), pl.ds(col, wide))
             pair = (
-                pltpu.make_async_copy(train.at[0, part], lat.at[t, part], in_sem.at[t, c, 0]),
-                pltpu.make_async_copy(other.at[0, part], oth.at[t, part], in_sem.at[t, c, 1]),
+                pltpu.make_async_copy(train.at[0, *at], lat.at[t, *at], in_sem.at[i, c, 0]),
+                pltpu.make_async_copy(other.at[0, *at], oth.at[t, *at], in_sem.at[i, c, 1]),
             )
             for copy in pair:
                 copy.start()
             loads.append(pair)
 
-    def remote(src, dst, send, recv, peer):
-        return pltpu.make_async_remote_copy(
-            src_ref=src, dst_ref=dst, send_sem=send, recv_sem=recv,
-            device_id=peer, device_id_type=MESH,
-        )
-
-    def local_sum(t):
-        acc = jnp.zeros((8, lat.shape[2]), jnp.float32)
-        for c in range(CHUNKS):
-            for copy in loads[t * CHUNKS + c]:
+    def local_sum(i):
+        t, col, wide = items[i]
+        cols = pl.ds(col, wide)
+        acc = jnp.zeros((8, wide), jnp.float32)
+        for c in range(CHUNKS):
+            for copy in loads[i * CHUNKS + c]:
                 copy.wait()
 
-            def add(i, acc, c=c):
-                r = pl.multiple_of(c * size + i * STEP, STEP)
-                v = lat[t, pl.ds(r, STEP), :] + oth[t, pl.ds(r, STEP), :].astype(jnp.float32)
-                lat[t, pl.ds(r, STEP), :] = v
+            def add(j, acc, c=c):
+                r = pl.ds(pl.multiple_of(c * size + j * STEP, STEP), STEP)
+                v = lat[t, r, cols] + oth[t, r, cols].astype(jnp.float32)
+                lat[t, r, cols] = v
                 v = v * v
                 for k in range(STEP // 8):
                     acc = acc + v[8 * k : 8 * k + 8]
                 return acc
 
             acc = lax.fori_loop(0, size // STEP, add, acc)
-        return jnp.sum(acc, axis=0, keepdims=True)
-
-    def spread(buf, send, recv):
+        sums[t, x, :, cols] = jnp.sum(acc, axis=0, keepdims=True)
+
+    def spread(piece, send, recv):
         copies = []
-        for k, peer in enumerate((right, left, across)):
-            copy = remote(buf.at[x], buf.at[x], send.at[k], recv.at[k], peer)
+        for k, peer in enumerate((across, right, left)):
+            copy = remote(piece, piece, send.at[k], recv.at[k], peer)
             copy.start()
             copies.append(copy)
         return copies
 
-    sums[0, x] = local_sum(0)
-    pl.semaphore_wait(barrier, len(row) + len(grid) * odd + core)
-    greet(grid + (twin,))
-    pending = spread(sums.at[0], sum_send.at[0], sum_recv.at[0])
+    sum_copies = []
+
+    def send_sum(i):
+        t, col, wide = items[i]
+        sum_copies.append(spread(sums.at[t, x, :, pl.ds(col, wide)], sum_send.at[i], sum_recv.at[i]))
+
+    local_sum(0)
+    pl.semaphore_wait(barrier, 3 + 2 * z_odd + 2 * y_odd + core)
+    send_sum(0)
+    raw_at = (pl.ds(0, RAW), pl.ds(items[0][1], items[0][2]))
+    raw_copies = []
+    for d, peer in enumerate((right, left)):
+        copy = remote(lat.at[0, *raw_at], raw.at[d], raw_send.at[d], raw_recv.at[d], peer)
+        copy.start()
+        raw_copies.append(copy)
+    for side, them in pairs:
+
+        @pl.when(side == 1)
+        def _(them=them):
+            for peer in them:
+                pl.semaphore_signal(answer_sem, inc=1, device_id=peer, device_id_type=MESH)
+
     rx[x] = rw_ref[...] * rg_ref[...]
-    rx_copies = spread(rx, rx_send, rx_recv)
-    sums[1, x] = local_sum(1)
-    later = spread(sums.at[1], sum_send.at[1], sum_recv.at[1])
+    rx_copies = spread(rx.at[x], rx_send, rx_recv)
+    for i in range(1, len(items)):
+        local_sum(i)
+        send_sum(i)
 
     outs, scales = (out_g, out_u), (scale_g, scale_u)
-    own = []
-    for t in range(2):
-        for copy in (pending, later)[t]:
+    own = {}
+    inverse = []
+    for i, (t, col, wide) in enumerate(items):
+        cols = pl.ds(col, wide)
+        for copy in sum_copies[i]:
             copy.wait()
-        total = sums[t, 0]
+        total = sums[t, 0, :, cols]
         for k in range(1, nx):
-            total = total + sums[t, k]
+            total = total + sums[t, k, :, cols]
         scale = jnp.sqrt(total)
-        scales[t][...] = scale
-        inv = jnp.broadcast_to(1.0 / scale, (STEP, lat.shape[2]))
-        for c in range(CHUNKS):
-
-            def narrow(i, carry, t=t, c=c, inv=inv):
-                r = pl.multiple_of(c * size + i * STEP, STEP)
-                w = pl.multiple_of(x * rows + c * size + i * STEP, STEP)
-                outs[t][0, pl.ds(w, STEP), :] = (lat[t, pl.ds(r, STEP), :] * inv).astype(jnp.bfloat16)
-                return carry
-
-            lax.fori_loop(0, size // STEP, narrow, 0)
-            where = pl.ds(pl.multiple_of(x * rows + c * size, size), size)
-            piece = outs[t].at[0, where]
-            for d, peer in enumerate((right, left)):
-                copy = remote(piece, piece, own_send.at[d, t, c], own_recv.at[d, t, c], peer)
-                copy.start()
-                own.append(copy)
-
-    answers = len(grid) * (1 - odd) + (1 - core)
+        scales[t][:, cols] = scale
+        inv = jnp.broadcast_to(1.0 / scale, (STEP, wide))
+        inverse.append(inv)
+        for c in range(CHUNKS):
+            skip = RAW if i == 0 and c == 0 else 0
+            for lo, hi in ((skip, size), (0, skip)):
+                if lo == hi:
+                    continue
+
+                def narrow(j, carry, t=t, c=c, inv=inv, cols=cols):
+                    r = pl.multiple_of(c * size + j * STEP, STEP)
+                    w = pl.multiple_of(x * rows + c * size + j * STEP, STEP)
+                    outs[t][0, pl.ds(w, STEP), cols] = (lat[t, pl.ds(r, STEP), cols] * inv).astype(jnp.bfloat16)
+                    return carry
+
+                lax.fori_loop(lo // STEP, hi // STEP, narrow, 0)
+                if lo == skip:
+                    where = pl.ds(pl.multiple_of(x * rows + c * size + skip, STEP), size - skip)
+                    piece = outs[t].at[0, where, cols]
+                    for d, peer in enumerate((right, left)):
+                        copy = remote(piece, piece, own_send.at[d, i, c], own_recv.at[d, i, c], peer)
+                        copy.start()
+                        own[d, i, c] = copy
+
+    cols = pl.ds(items[0][1], items[0][2])
+    for d, source in enumerate((step(x, -1, nx), step(x, 1, nx))):
+        raw_copies[d].wait_recv()
+
+        def narrow_raw(j, carry, d=d, source=source):
+            r = pl.multiple_of(j * STEP, STEP)
+            w = pl.multiple_of(source * rows + j * STEP, STEP)
+            outs[0][0, pl.ds(w, STEP), cols] = (raw[d, pl.ds(r, STEP), :] * inverse[0]).astype(jnp.bfloat16)
+            return carry
+
+        lax.fori_loop(0, RAW // STEP, narrow_raw, 0)
+
+    answers = 2 * (1 - z_odd) + 2 * (1 - y_odd) + (1 - core)
 
     @pl.when(answers > 0)
     def _():
-        pl.semaphore_wait(barrier, answers)
+        pl.semaphore_wait(answer_sem, answers)
 
     for copy in rx_copies:
         copy.wait()
@@ -178,10 +226,12 @@
 
     fwd = []
     half = CHUNKS // 2
+    by_tensor = [[i for i, item in enumerate(items) if item[0] == t] for t in range(2)]
     for t in range(2):
         for c in range(CHUNKS):
             d = 0 if c < half else 1
-            own[(t * CHUNKS + c) * 2 + d].wait_recv()
+            for i in by_tensor[t]:
+                own[d, i, c].wait_recv()
             source = step(x, -1, nx) if d == 0 else step(x, 1, nx)
             where = pl.ds(pl.multiple_of(source * rows + c * size, size), size)
             piece = outs[t].at[0, where]
@@ -191,8 +241,9 @@
     for t in range(2):
         for c in range(CHUNKS):
             d = 0 if c < half else 1
-            own[(t * CHUNKS + c) * 2 + 1 - d].wait_recv()
-    for copy in own:
+            for i in by_tensor[t]:
+                own[1 - d, i, c].wait_recv()
+    for copy in raw_copies + list(own.values()):
         copy.wait_send()
     for copy in fwd:
         copy.wait()
@@ -222,6 +273,7 @@
     hbm = pl.BlockSpec(memory_space=pltpu.HBM)
     vmem = pl.BlockSpec(memory_space=pltpu.VMEM)
     dma = pltpu.SemaphoreType.DMA
+    count = SPLIT + 1
     out = pl.pallas_call(
         functools.partial(kernel, dims),
         out_shape=(
@@ -237,13 +289,15 @@
             pltpu.VMEM((2, rows, width), jnp.float32),
             pltpu.VMEM((2, rows, width), jnp.bfloat16),
             pltpu.VMEM((2, nx, 1, width), jnp.float32),
+            pltpu.VMEM((2, RAW, width // SPLIT), jnp.float32),
             pltpu.VMEM((nx, 1, rows), jnp.float32),
             pltpu.VMEM((ny * nc, 1, whole), jnp.float32),
             pltpu.VMEM((nz, ny * nc, whole), jnp.float32),
-            dma((2, CHUNKS, 2)),
-            dma((2, 3)), dma((2, 3)), dma((3,)), dma((3,)),
-            dma((2, 2, CHUNKS)), dma((2, 2, CHUNKS)), dma((2, CHUNKS)), dma((2, CHUNKS)),
+            dma((count, CHUNKS, 2)),
+            dma((count, 3)), dma((count, 3)), dma((2,)), dma((2,)), dma((3,)), dma((3,)),
+            dma((2, count, CHUNKS)), dma((2, count, CHUNKS)), dma((2, CHUNKS)), dma((2, CHUNKS)),
             dma((4,)), dma((4,)), dma((2, 4)), dma((2, 4)),
+            pltpu.SemaphoreType.REGULAR,
         ],
         compiler_params=pltpu.CompilerParams(
             collective_id=0, has_side_effects=True, vmem_limit_bytes=48 << 20

time: 88.1 us -> 81.9 us (0.930); the launches traced: 87.9 us -> 80.4 us
  Pallas kernels: 87.3 us -> 79.8 us
    pallas_call x1, Pallas kernels: 83.8 us -> 76.3 us  [body(): pl.pallas_call(functools.partial(kernel, dims), out_shape=(pltpu.VMEM((1,...]
where the time goes in v3:
time: 81.9 us; the launch traced here: 80.4 us
  Pallas kernels  79.8 us (97%)
    pallas_call x1, Pallas kernels, body(): pl.pallas_call(functools.partial(kernel, dims), out_shape=(pltpu.VMEM((1,...  76.3 us
    pallas_call x1, Pallas kernels, body(): pl.pallas_call(write_out, out_shape=tuple((jax.ShapeDtypeStruct(o.shape,...  3.53 us

profile of v3, /device:TPU:8, one launch (start us, length us, event | category | flops | bytes accessed | tf_op | source)
XLA Modules:
  0.0 80.4 jit_solution(13543611020648782601)
XLA Ops:
  0.6 76.3 %ring.1 = (bf16[1,2048,1024]{2,1,0:T(8,128)(2,1)S(1)}, bf16[1,2048,1024]{2,1,0:T(8,128)(2,1)S(1)}, f32[1,1024]{1,0:T(1,128)S(1)}, f32[1,1024]{1,0:T(1,128)S(1)}, bf16[64,2048]{1,0:T(8,128)(2,1)S(1)}) custom-call(f32[1,512,1024]{2,1,0:T(8,128)} %tg_hbm.1, bf16[1,512,1024]{2,1,0:T(8,128)(2,1)} %og_hbm.1, f32[1,512,1024]{2,1,0:T(8,128)} %tu_hbm.1, ...), custom_call_target="tpu_custom_call" | custom-call | tf_op jit(solution)/shard_map/ring/pallas_call | solution.py:277
  76.9 3.5 %write_out.1 = (bf16[1,2048,1024]{2,1,0:T(8,128)(2,1)}, bf16[1,2048,1024]{2,1,0:T(8,128)(2,1)}, f32[1,1024]{1,0:T(1,128)}, f32[1,1024]{1,0:T(1,128)}, bf16[64,2048]{1,0:T(8,128)(2,1)}) custom-call(bf16[1,2048,1024]{2,1,0:T(8,128)(2,1)S(1)} %get-tuple-element.15.refs_0_, bf16[1,2048,1024]{2,1,0:T(8,128)(2,1)S(1)} %get-tuple-element.16.refs_1_, ...), custom_call_target="tpu_custom_call" | custom-call | tf_op jit(solution)/shard_map/write_out/pallas_call | solution.py:307

commit v4 on v3

v4 whole, which is shorter than its diff:
```python
import functools

import jax
import jax.numpy as jnp
from jax import lax
from jax.experimental import pallas as pl
from jax.experimental.pallas import tpu as pltpu
from jax.sharding import PartitionSpec as P

MESH = pl.DeviceIdType.MESH
STEP = 16
PARTS = 2
RAW = 64
FIRST = 256
PIECES = 2


def kernel(
    dims,
    tg_hbm, og_hbm, tu_hbm, ou_hbm, rw_hbm, rg_hbm,
    out_g, out_u, scale_g, scale_u, router,
    lat, oth, sums, raw, rin, rx, plane, zring,
    in_sem, rin_sem, sum_send, sum_recv, raw_send, raw_recv, rx_send, rx_recv,
    own_send, near_recv, rest_recv, fwd_send, fwd_recv,
    pl_send, pl_recv, z_send, z_recv, answer_sem,
):
    nx, ny, nz, nc, rows = dims
    width = lat.shape[2]
    half = rows // 2
    x = lax.axis_index("fsdp")
    e = lax.axis_index("ep")
    core = lax.rem(e, nc)
    y = lax.rem(lax.div(e, nc), ny)
    z = lax.div(e, nc * ny)
    y_odd, z_odd = lax.rem(y, 2), lax.rem(z, 2)

    def ep_of(zz, yy, cc):
        return (zz * ny + yy) * nc + cc

    def step(v, d, n):
        return lax.rem(v + d + n, n)

    def remote(src, dst, send, recv, peer):
        return pltpu.make_async_remote_copy(
            src_ref=src, dst_ref=dst, send_sem=send, recv_sem=recv,
            device_id=peer, device_id_type=MESH,
        )

    def wait_bytes(ref, sem):
        pltpu.make_async_copy(ref, ref, sem).wait()

    right = (e, step(x, 1, nx))
    left = (e, step(x, -1, nx))
    across = (e, step(x, 2, nx))
    y_up = (ep_of(z, step(y, 1, ny), core), x)
    y_dn = (ep_of(z, step(y, -1, ny), core), x)
    z_up = (ep_of(step(z, 1, nz), y, core), x)
    z_dn = (ep_of(step(z, -1, nz), y, core), x)
    twin = (ep_of(z, y, step(core, 1, nc)), x)

    barrier = pltpu.get_barrier_semaphore()
    for peer in (across, right, left):
        pl.semaphore_signal(barrier, inc=1, device_id=peer, device_id_type=MESH)
    pairs = ((z_odd, (z_up, z_dn)), (y_odd, (y_up, y_dn)), (core, (twin,)))

    items = ((0, 0, FIRST), (0, FIRST, width - FIRST), (1, 0, width))
    loads = []
    for i, (t, col, wide) in enumerate(items):
        train, other = ((tg_hbm, og_hbm), (tu_hbm, ou_hbm))[t]
        for h in range(2):
            at = (pl.ds(h * half, half), pl.ds(col, wide))
            pair = (
                pltpu.make_async_copy(train.at[0, *at], lat.at[t, *at], in_sem.at[i, h, 0]),
                pltpu.make_async_copy(other.at[0, *at], oth.at[t, *at], in_sem.at[i, h, 1]),
            )
            for copy in pair:
                copy.start(priority=min(i, 1))
            loads.append(pair)
        if i == 0:
            pltpu.make_async_copy(rw_hbm, rin.at[0], rin_sem).start()
            pltpu.make_async_copy(rg_hbm, rin.at[1], rin_sem).start()

    for side, them in pairs:

        @pl.when(side == 0)
        def _(them=them):
            for peer in them:
                pl.semaphore_signal(barrier, inc=1, device_id=peer, device_id_type=MESH)

    def local_sum(i):
        t, col, wide = items[i]
        cols = pl.ds(col, wide)
        acc = jnp.zeros((8, wide), jnp.float32)
        for h in range(2):
            for copy in loads[2 * i + h]:
                copy.wait()

            def add(j, acc, h=h):
                r = pl.ds(pl.multiple_of(h * half + j * STEP, STEP), STEP)
                v = lat[t, r, cols] + oth[t, r, cols].astype(jnp.float32)
                lat[t, r, cols] = v
                v = v * v
                for k in range(STEP // 8):
                    acc = acc + v[8 * k : 8 * k + 8]
                return acc

            acc = lax.fori_loop(0, half // STEP, add, acc)
        sums[t, x, :, cols] = jnp.sum(acc, axis=0, keepdims=True)

    def spread(piece, send, recv):
        for peer in (across, right, left):
            remote(piece, piece, send, recv, peer).start()

    def send_sum(i):
        t, col, wide = items[i]
        spread(sums.at[t, x, :, pl.ds(col, wide)], sum_send, sum_recv.at[i])

    local_sum(0)
    pl.semaphore_wait(barrier, 3 + 2 * z_odd + 2 * y_odd + core)
    send_sum(0)
    for d, peer in enumerate((right, left)):
        remote(lat.at[0, pl.ds(0, RAW), pl.ds(0, FIRST)], raw.at[d], raw_send, raw_recv, peer).start()
    for side, them in pairs:

        @pl.when(side == 1)
        def _(them=them):
            for peer in them:
                pl.semaphore_signal(answer_sem, inc=1, device_id=peer, device_id_type=MESH)

    for i in range(1, len(items)):
        local_sum(i)
        send_sum(i)
    wait_bytes(rin, rin_sem)
    rx[x] = rin[0] * rin[1]
    spread(rx.at[x], rx_send, rx_recv)

    outs, scales = (out_g, out_u), (scale_g, scale_u)
    inverse = []
    size = half // PIECES
    for i, (t, col, wide) in enumerate(items):
        cols = pl.ds(col, wide)
        wait_bytes(sums.at[t, pl.ds(0, nx - 1), :, cols], sum_recv.at[i])
        total = sums[t, 0, :, cols]
        for k in range(1, nx):
            total = total + sums[t, k, :, cols]
        scale = jnp.sqrt(total)
        scales[t][:, cols] = scale
        inv = jnp.broadcast_to(1.0 / scale, (STEP, wide))
        inverse.append(inv)
        for c in range(2 * PIECES):
            h = c // PIECES
            skip = RAW if i == 0 and c == 0 else 0
            for lo, hi in ((skip, size), (0, skip)):
                if lo == hi:
                    continue

                def narrow(j, carry, t=t, c=c, inv=inv, cols=cols):
                    r = pl.multiple_of(c * size + j * STEP, STEP)
                    w = pl.multiple_of(x * rows + c * size + j * STEP, STEP)
                    outs[t][0, pl.ds(w, STEP), cols] = (lat[t, pl.ds(r, STEP), cols] * inv).astype(jnp.bfloat16)
                    return carry

                lax.fori_loop(lo // STEP, hi // STEP, narrow, 0)
                if lo == skip:
                    where = pl.ds(pl.multiple_of(x * rows + c * size + skip, STEP), size - skip)
                    piece = outs[t].at[0, where, cols]
                    for d, peer in enumerate((right, left)):
                        recv = near_recv.at[d, t] if h == d else rest_recv.at[d]
                        remote(piece, piece, own_send, recv, peer).start()

    wait_bytes(raw, raw_recv)
    sides = (step(x, -1, nx), step(x, 1, nx))
    for d, source in enumerate(sides):

        def narrow_raw(j, carry, d=d, source=source):
            r = pl.multiple_of(j * STEP, STEP)
            w = pl.multiple_of(source * rows + j * STEP, STEP)
            outs[0][0, pl.ds(w, STEP), pl.ds(0, FIRST)] = (raw[d, pl.ds(r, STEP), :] * inverse[0]).astype(jnp.bfloat16)
            return carry

        lax.fori_loop(0, RAW // STEP, narrow_raw, 0)

    answers = 2 * (1 - z_odd) + 2 * (1 - y_odd) + (1 - core)

    @pl.when(answers > 0)
    def _():
        pl.semaphore_wait(answer_sem, answers)

    wait_bytes(rx.at[pl.ds(0, nx - 1)], rx_recv)
    mine = y * nc + core
    plane[mine] = jnp.concatenate([rx[k] for k in range(nx)], axis=1)
    first = remote(plane.at[mine], plane.at[mine], pl_send, pl_recv.at[0], twin)
    first.start()
    first.wait_recv()
    near = pl.ds(y * nc, nc)
    ups = remote(plane.at[near], plane.at[near], pl_send, pl_recv.at[1], y_up)
    dns = remote(plane.at[near], plane.at[near], pl_send, pl_recv.at[2], y_dn)
    ups.start()
    dns.start()
    ups.wait_recv()
    dns.wait_recv()
    from_dn = pl.ds(step(y, -1, ny) * nc, nc)
    far = remote(plane.at[from_dn], plane.at[from_dn], pl_send, pl_recv.at[3], y_up)
    far.start()
    far.wait_recv()
    zring[z] = jnp.concatenate([plane[k] for k in range(ny * nc)], axis=0)
    hops_up, hops_dn = nz // 2, nz - 1 - nz // 2
    for s in range(hops_up):
        at = step(z, -s, nz)
        moves = [remote(zring.at[at], zring.at[at], z_send, z_recv.at[s], z_up)]
        if s < hops_dn:
            at = step(z, s, nz)
            moves.append(remote(zring.at[at], zring.at[at], z_send, z_recv.at[hops_up + s], z_dn))
        for copy in moves:
            copy.start()
        for copy in moves:
            copy.wait_recv()
    for k in range(nz // 2):
        both = jnp.concatenate([zring[2 * k], zring[2 * k + 1]], axis=0)
        router[pl.ds(2 * k * ny * nc, 2 * ny * nc), :] = both.astype(jnp.bfloat16)

    sent_raw = RAW * FIRST // width
    for t in range(2):
        for d, source in enumerate(sides):
            count = half - (sent_raw if t == 0 and d == 0 else 0)
            wait_bytes(outs[t].at[0, pl.ds(0, count)], near_recv.at[d, t])
            where = pl.ds(pl.multiple_of(source * rows + d * half, half), half)
            piece = outs[t].at[0, where]
            remote(piece, piece, fwd_send, fwd_recv, (right, left)[d]).start()
    for d in range(2):
        count = 2 * half - (sent_raw if d == 1 else 0)
        wait_bytes(out_g.at[0, pl.ds(0, count)], rest_recv.at[d])
    wait_bytes(sums.at[:, pl.ds(0, nx - 1)], sum_send)
    wait_bytes(rx.at[pl.ds(0, nx - 1)], rx_send)
    wait_bytes(raw, raw_send)
    wait_bytes(plane.at[pl.ds(0, 1 + 3 * nc)], pl_send)
    wait_bytes(zring.at[pl.ds(0, nz - 1)], z_send)
    wait_bytes(out_g.at[0, pl.ds(0, 2 * (2 * rows - sent_raw))], own_send)
    wait_bytes(out_g.at[0, pl.ds(0, 4 * half)], fwd_send)
    wait_bytes(out_g.at[0, pl.ds(0, 4 * half)], fwd_recv)


def write_out(*refs):
    held, outs, sem = refs[:5], refs[5:10], refs[10]
    copies = []
    for k in range(2):
        size = held[k].shape[1] // PARTS
        for p in range(PARTS):
            part = (0, pl.ds(p * size, size))
            copies.append(pltpu.make_async_copy(held[k].at[part], outs[k].at[part], sem.at[k * PARTS + p]))
    for k in range(2, 5):
        copies.append(pltpu.make_async_copy(held[k], outs[k], sem.at[2 * PARTS + k - 2]))
    for copy in copies:
        copy.start()
    for copy in copies:
        copy.wait()


def body(dims, train_gate, other_gate, train_up, other_up, router_weight, router_gain):
    nx, ny, nz, nc, rows = dims
    width = train_gate.shape[2]
    whole = nx * rows
    experts = ny * nz * nc
    hbm = pl.BlockSpec(memory_space=pltpu.HBM)
    vmem = pl.BlockSpec(memory_space=pltpu.VMEM)
    dma = pltpu.SemaphoreType.DMA
    out = pl.pallas_call(
        functools.partial(kernel, dims),
        out_shape=(
            pltpu.VMEM((1, whole, width), jnp.bfloat16),
            pltpu.VMEM((1, whole, width), jnp.bfloat16),
            pltpu.VMEM((1, width), jnp.float32),
            pltpu.VMEM((1, width), jnp.float32),
            pltpu.VMEM((experts, whole), jnp.bfloat16),
        ),
        in_specs=[hbm] * 6,
        out_specs=(vmem,) * 5,
        scratch_shapes=[
            pltpu.VMEM((2, rows, width), jnp.float32),
            pltpu.VMEM((2, rows, width), jnp.bfloat16),
            pltpu.VMEM((2, nx, 1, width), jnp.float32),
            pltpu.VMEM((2, RAW, FIRST), jnp.float32),
            pltpu.VMEM((2, 1, rows), jnp.float32),
            pltpu.VMEM((nx, 1, rows), jnp.float32),
            pltpu.VMEM((ny * nc, 1, whole), jnp.float32),
            pltpu.VMEM((nz, ny * nc, whole), jnp.float32),
            dma((3, 2, 2)), dma(()), dma(()), dma((3,)), dma(()), dma(()), dma(()), dma(()),
            dma(()), dma((2, 2)), dma((2,)), dma(()), dma(()),
            dma(()), dma((4,)), dma(()), dma((nz - 1,)),
            pltpu.SemaphoreType.REGULAR,
        ],
        compiler_params=pltpu.CompilerParams(
            collective_id=0, has_side_effects=True, vmem_limit_bytes=48 << 20
        ),
        name="ring",
    )(train_gate, other_gate, train_up, other_up, router_weight.T, router_gain[None, :])
    ready_gate, ready_up, scale_gate, scale_up, router = pl.pallas_call(
        write_out,
        out_shape=tuple(pltpu.HBM(o.shape, o.dtype) for o in out),
        in_specs=[vmem] * 5,
        out_specs=(hbm,) * 5,
        scratch_shapes=[dma((2 * PARTS + 3,))],
        compiler_params=pltpu.CompilerParams(vmem_limit_bytes=4 << 20),
        name="write_out",
    )(*out)
    return ready_gate, ready_up, scale_gate, scale_up, router.T


def solution(mesh):
    placed = (
        P("ep", "fsdp", None),
        P("ep", "fsdp", None),
        P("ep", "fsdp", None),
        P("ep", "fsdp", None),
        P("fsdp", "ep"),
        P("fsdp"),
    )
    nx, ep = mesh.shape["fsdp"], mesh.shape["ep"]
    dims = (nx, 4, ep // 8, 2, 2048 // nx)
    return jax.shard_map(
        functools.partial(body, dims),
        mesh=mesh,
        in_specs=placed,
        out_specs=(P("ep", None, None), P("ep", None, None), P("ep", None), P("ep", None), P()),
        check_vma=False,
    )
```

time: 81.9 us -> 80 us (0.977)
  Pallas kernels: 79.8 us -> 78.2 us
    pallas_call x1, Pallas kernels: 76.3 us -> 74.8 us  [body(): pl.pallas_call(functools.partial(kernel, dims), out_shape=(pltpu.VMEM((1,...]
where the time goes in v4:
time: 80 us; the launch traced here: 78.8 us
  Pallas kernels  78.2 us (98%)
    pallas_call x1, Pallas kernels, body(): pl.pallas_call(functools.partial(kernel, dims), out_shape=(pltpu.VMEM((1,...  74.8 us
    pallas_call x1, Pallas kernels, body(): pl.pallas_call(write_out, out_shape=tuple((pltpu.HBM(o.shape, o.dtype) fo...  3.42 us

profile of v4, /device:TPU:8, one launch (start us, length us, event | category | flops | bytes accessed | tf_op | source)
XLA Modules:
  0.0 78.8 jit_solution(9529103403744926227)
XLA Ops:
  0.6 74.8 %ring.1 = (bf16[1,2048,1024]{2,1,0:T(8,128)(2,1)S(1)}, bf16[1,2048,1024]{2,1,0:T(8,128)(2,1)S(1)}, f32[1,1024]{1,0:T(1,128)S(1)}, f32[1,1024]{1,0:T(1,128)S(1)}, bf16[64,2048]{1,0:T(8,128)(2,1)S(1)}) custom-call(f32[1,512,1024]{2,1,0:T(8,128)} %tg_hbm.1, bf16[1,512,1024]{2,1,0:T(8,128)(2,1)} %og_hbm.1, f32[1,512,1024]{2,1,0:T(8,128)} %tu_hbm.1, ...), custom_call_target="tpu_custom_call" | custom-call | tf_op jit(solution)/shard_map/ring/pallas_call | solution.py:267
  75.4 3.4 %write_out.1 = (bf16[1,2048,1024]{2,1,0:T(8,128)(2,1)}, bf16[1,2048,1024]{2,1,0:T(8,128)(2,1)}, f32[1,1024]{1,0:T(1,128)}, f32[1,1024]{1,0:T(1,128)}, bf16[64,2048]{1,0:T(8,128)(2,1)}) custom-call(bf16[1,2048,1024]{2,1,0:T(8,128)(2,1)S(1)} %get-tuple-element.15.refs_0_, bf16[1,2048,1024]{2,1,0:T(8,128)(2,1)S(1)} %get-tuple-element.16.refs_1_, ...), custom_call_target="tpu_custom_call" | custom-call | tf_op jit(solution)/shard_map/write_out/pallas_call | solution.py:297

commit v5 on v4

--- a/solution.py
+++ b/solution.py
@@ -32,7 +32,6 @@
     core = lax.rem(e, nc)
     y = lax.rem(lax.div(e, nc), ny)
     z = lax.div(e, nc * ny)
-    y_odd, z_odd = lax.rem(y, 2), lax.rem(z, 2)
 
     def ep_of(zz, yy, cc):
         return (zz * ny + yy) * nc + cc
@@ -61,7 +60,13 @@
     barrier = pltpu.get_barrier_semaphore()
     for peer in (across, right, left):
         pl.semaphore_signal(barrier, inc=1, device_id=peer, device_id_type=MESH)
-    pairs = ((z_odd, (z_up, z_dn)), (y_odd, (y_up, y_dn)), (core, (twin,)))
+    z_lo, z_hi, y_lo, y_hi = z == 0, z == nz - 1, y == 0, y == ny - 1
+    pairs = (
+        (z_up, jnp.logical_not(z_hi)), (z_dn, z_lo),
+        (y_up, jnp.logical_not(y_hi)), (y_dn, y_lo),
+        (twin, core == 0),
+    )
+    greeted = sum(g.astype(jnp.int32) for _, g in pairs)
 
     items = ((0, 0, FIRST), (0, FIRST, width - FIRST), (1, 0, width))
     loads = []
@@ -80,12 +85,11 @@
             pltpu.make_async_copy(rw_hbm, rin.at[0], rin_sem).start()
             pltpu.make_async_copy(rg_hbm, rin.at[1], rin_sem).start()
 
-    for side, them in pairs:
-
-        @pl.when(side == 0)
-        def _(them=them):
-            for peer in them:
-                pl.semaphore_signal(barrier, inc=1, device_id=peer, device_id_type=MESH)
+    for peer, greets in pairs:
+
+        @pl.when(greets)
+        def _(peer=peer):
+            pl.semaphore_signal(barrier, inc=1, device_id=peer, device_id_type=MESH)
 
     def local_sum(i):
         t, col, wide = items[i]
@@ -116,16 +120,15 @@
         spread(sums.at[t, x, :, pl.ds(col, wide)], sum_send, sum_recv.at[i])
 
     local_sum(0)
-    pl.semaphore_wait(barrier, 3 + 2 * z_odd + 2 * y_odd + core)
+    pl.semaphore_wait(barrier, 3 + len(pairs) - greeted)
     send_sum(0)
-    for d, peer in enumerate((right, left)):
+    for d, peer in list(enumerate((right, left)))[: 2 * (RAW > 0)]:
         remote(lat.at[0, pl.ds(0, RAW), pl.ds(0, FIRST)], raw.at[d], raw_send, raw_recv, peer).start()
-    for side, them in pairs:
-
-        @pl.when(side == 1)
-        def _(them=them):
-            for peer in them:
-                pl.semaphore_signal(answer_sem, inc=1, device_id=peer, device_id_type=MESH)
+    for peer, greets in pairs:
+
+        @pl.when(jnp.logical_not(greets))
+        def _(peer=peer):
+            pl.semaphore_signal(answer_sem, inc=1, device_id=peer, device_id_type=MESH)
 
     for i in range(1, len(items)):
         local_sum(i)
@@ -168,7 +171,8 @@
                         recv = near_recv.at[d, t] if h == d else rest_recv.at[d]
                         remote(piece, piece, own_send, recv, peer).start()
 
-    wait_bytes(raw, raw_recv)
+    if RAW:
+        wait_bytes(raw, raw_recv)
     sides = (step(x, -1, nx), step(x, 1, nx))
     for d, source in enumerate(sides):
 
@@ -180,11 +184,9 @@
 
         lax.fori_loop(0, RAW // STEP, narrow_raw, 0)
 
-    answers = 2 * (1 - z_odd) + 2 * (1 - y_odd) + (1 - core)
-
-    @pl.when(answers > 0)
+    @pl.when(greeted > 0)
     def _():
-        pl.semaphore_wait(answer_sem, answers)
+        pl.semaphore_wait(answer_sem, greeted)
 
     wait_bytes(rx.at[pl.ds(0, nx - 1)], rx_recv)
     mine = y * nc + core
@@ -232,7 +234,8 @@
         wait_bytes(out_g.at[0, pl.ds(0, count)], rest_recv.at[d])
     wait_bytes(sums.at[:, pl.ds(0, nx - 1)], sum_send)
     wait_bytes(rx.at[pl.ds(0, nx - 1)], rx_send)
-    wait_bytes(raw, raw_send)
+    if RAW:
+        wait_bytes(raw, raw_send)
     wait_bytes(plane.at[pl.ds(0, 1 + 3 * nc)], pl_send)
     wait_bytes(zring.at[pl.ds(0, nz - 1)], z_send)
     wait_bytes(out_g.at[0, pl.ds(0, 2 * (2 * rows - sent_raw))], own_send)
@@ -279,7 +282,7 @@
             pltpu.VMEM((2, rows, width), jnp.float32),
             pltpu.VMEM((2, rows, width), jnp.bfloat16),
             pltpu.VMEM((2, nx, 1, width), jnp.float32),
-            pltpu.VMEM((2, RAW, FIRST), jnp.float32),
+            pltpu.VMEM((2, max(RAW, STEP), FIRST), jnp.float32),
             pltpu.VMEM((2, 1, rows), jnp.float32),
             pltpu.VMEM((nx, 1, rows), jnp.float32),
             pltpu.VMEM((ny * nc, 1, whole), jnp.float32),

time: 80 us -> 78.9 us (0.986); the launches traced: 78.8 us -> 78.9 us
  no operation moved by 1% of the time
where the time goes in v5:
time: 78.9 us
  Pallas kernels  78.2 us (99%)
    pallas_call x1, Pallas kernels, body(): pl.pallas_call(functools.partial(kernel, dims), out_shape=(pltpu.VMEM((1,...  74.8 us
    pallas_call x1, Pallas kernels, body(): pl.pallas_call(write_out, out_shape=tuple((pltpu.HBM(o.shape, o.dtype) fo...  3.42 us

profile of v5, /device:TPU:8, one launch (start us, length us, event | category | flops | bytes accessed | tf_op | source)
XLA Modules:
  0.0 78.9 jit_solution(2112660938004072144)
XLA Ops:
  0.6 74.8 %ring.1 = (bf16[1,2048,1024]{2,1,0:T(8,128)(2,1)S(1)}, bf16[1,2048,1024]{2,1,0:T(8,128)(2,1)S(1)}, f32[1,1024]{1,0:T(1,128)S(1)}, f32[1,1024]{1,0:T(1,128)S(1)}, bf16[64,2048]{1,0:T(8,128)(2,1)S(1)}) custom-call(f32[1,512,1024]{2,1,0:T(8,128)} %tg_hbm.1, bf16[1,512,1024]{2,1,0:T(8,128)(2,1)} %og_hbm.1, f32[1,512,1024]{2,1,0:T(8,128)} %tu_hbm.1, ...), custom_call_target="tpu_custom_call" | custom-call | tf_op jit(solution)/shard_map/ring/pallas_call | solution.py:270
  75.4 3.4 %write_out.1 = (bf16[1,2048,1024]{2,1,0:T(8,128)(2,1)}, bf16[1,2048,1024]{2,1,0:T(8,128)(2,1)}, f32[1,1024]{1,0:T(1,128)}, f32[1,1024]{1,0:T(1,128)}, bf16[64,2048]{1,0:T(8,128)(2,1)}) custom-call(bf16[1,2048,1024]{2,1,0:T(8,128)(2,1)S(1)} %get-tuple-element.15.refs_0_, bf16[1,2048,1024]{2,1,0:T(8,128)(2,1)S(1)} %get-tuple-element.16.refs_1_, ...), custom_call_target="tpu_custom_call" | custom-call | tf_op jit(solution)/shard_map/write_out/pallas_call | solution.py:300

commit v6 on v5

--- a/solution.py
+++ b/solution.py
@@ -10,9 +10,9 @@
 MESH = pl.DeviceIdType.MESH
 STEP = 16
 PARTS = 2
-RAW = 64
+RAW = 96
 FIRST = 256
-PIECES = 2
+PIECES = 1
 
 
 def kernel(
@@ -79,7 +79,7 @@
                 pltpu.make_async_copy(other.at[0, *at], oth.at[t, *at], in_sem.at[i, h, 1]),
             )
             for copy in pair:
-                copy.start(priority=min(i, 1))
+                copy.start()
             loads.append(pair)
         if i == 0:
             pltpu.make_async_copy(rw_hbm, rin.at[0], rin_sem).start()
@@ -122,7 +122,7 @@
     local_sum(0)
     pl.semaphore_wait(barrier, 3 + len(pairs) - greeted)
     send_sum(0)
-    for d, peer in list(enumerate((right, left)))[: 2 * (RAW > 0)]:
+    for d, peer in enumerate((right, left)):
         remote(lat.at[0, pl.ds(0, RAW), pl.ds(0, FIRST)], raw.at[d], raw_send, raw_recv, peer).start()
     for peer, greets in pairs:
 
@@ -171,8 +171,7 @@
                         recv = near_recv.at[d, t] if h == d else rest_recv.at[d]
                         remote(piece, piece, own_send, recv, peer).start()
 
-    if RAW:
-        wait_bytes(raw, raw_recv)
+    wait_bytes(raw, raw_recv)
     sides = (step(x, -1, nx), step(x, 1, nx))
     for d, source in enumerate(sides):
 
@@ -234,8 +233,7 @@
         wait_bytes(out_g.at[0, pl.ds(0, count)], rest_recv.at[d])
     wait_bytes(sums.at[:, pl.ds(0, nx - 1)], sum_send)
     wait_bytes(rx.at[pl.ds(0, nx - 1)], rx_send)
-    if RAW:
-        wait_bytes(raw, raw_send)
+    wait_bytes(raw, raw_send)
     wait_bytes(plane.at[pl.ds(0, 1 + 3 * nc)], pl_send)
     wait_bytes(zring.at[pl.ds(0, nz - 1)], z_send)
     wait_bytes(out_g.at[0, pl.ds(0, 2 * (2 * rows - sent_raw))], own_send)
@@ -282,7 +280,7 @@
             pltpu.VMEM((2, rows, width), jnp.float32),
             pltpu.VMEM((2, rows, width), jnp.bfloat16),
             pltpu.VMEM((2, nx, 1, width), jnp.float32),
-            pltpu.VMEM((2, max(RAW, STEP), FIRST), jnp.float32),
+            pltpu.VMEM((2, RAW, FIRST), jnp.float32),
             pltpu.VMEM((2, 1, rows), jnp.float32),
             pltpu.VMEM((nx, 1, rows), jnp.float32),
             pltpu.VMEM((ny * nc, 1, whole), jnp.float32),

time: 78.9 us -> 78.6 us (level)
  no operation moved by 1% of the time
where the time goes in v6:
time: 78.6 us; the launch traced here: 78.5 us
  Pallas kernels  77.9 us (99%)
    pallas_call x1, Pallas kernels, body(): pl.pallas_call(functools.partial(kernel, dims), out_shape=(pltpu.VMEM((1,...  74.5 us
    pallas_call x1, Pallas kernels, body(): pl.pallas_call(write_out, out_shape=tuple((pltpu.HBM(o.shape, o.dtype) fo...  3.42 us

profile of v6, /device:TPU:8, one launch (start us, length us, event | category | flops | bytes accessed | tf_op | source)
XLA Modules:
  0.0 78.5 jit_solution(8028831762099508563)
XLA Ops:
  0.6 74.5 %ring.1 = (bf16[1,2048,1024]{2,1,0:T(8,128)(2,1)S(1)}, bf16[1,2048,1024]{2,1,0:T(8,128)(2,1)S(1)}, f32[1,1024]{1,0:T(1,128)S(1)}, f32[1,1024]{1,0:T(1,128)S(1)}, bf16[64,2048]{1,0:T(8,128)(2,1)S(1)}) custom-call(f32[1,512,1024]{2,1,0:T(8,128)} %tg_hbm.1, bf16[1,512,1024]{2,1,0:T(8,128)(2,1)} %og_hbm.1, f32[1,512,1024]{2,1,0:T(8,128)} %tu_hbm.1, ...), custom_call_target="tpu_custom_call" | custom-call | tf_op jit(solution)/shard_map/ring/pallas_call | solution.py:268
  75.1 3.4 %write_out.1 = (bf16[1,2048,1024]{2,1,0:T(8,128)(2,1)}, bf16[1,2048,1024]{2,1,0:T(8,128)(2,1)}, f32[1,1024]{1,0:T(1,128)}, f32[1,1024]{1,0:T(1,128)}, bf16[64,2048]{1,0:T(8,128)(2,1)}) custom-call(bf16[1,2048,1024]{2,1,0:T(8,128)(2,1)S(1)} %get-tuple-element.15.refs_0_, bf16[1,2048,1024]{2,1,0:T(8,128)(2,1)S(1)} %get-tuple-element.16.refs_1_, ...), custom_call_target="tpu_custom_call" | custom-call | tf_op jit(solution)/shard_map/write_out/pallas_call | solution.py:298

commit v7 on v6

--- a/solution.py
+++ b/solution.py
@@ -72,15 +72,17 @@
     loads = []
     for i, (t, col, wide) in enumerate(items):
         train, other = ((tg_hbm, og_hbm), (tu_hbm, ou_hbm))[t]
-        for h in range(2):
-            at = (pl.ds(h * half, half), pl.ds(col, wide))
+        parts = 2 if i == 0 else 1
+        deep = rows // parts
+        for h in range(parts):
+            at = (pl.ds(h * deep, deep), pl.ds(col, wide))
             pair = (
-                pltpu.make_async_copy(train.at[0, *at], lat.at[t, *at], in_sem.at[i, h, 0]),
-                pltpu.make_async_copy(other.at[0, *at], oth.at[t, *at], in_sem.at[i, h, 1]),
+                pltpu.make_async_copy(train.at[0, *at], lat.at[t, *at], in_sem.at[i + h if i == 0 else i + 1, 0]),
+                pltpu.make_async_copy(other.at[0, *at], oth.at[t, *at], in_sem.at[i + h if i == 0 else i + 1, 1]),
             )
             for copy in pair:
                 copy.start()
-            loads.append(pair)
+            loads.append((i, h, deep, pair))
         if i == 0:
             pltpu.make_async_copy(rw_hbm, rin.at[0], rin_sem).start()
             pltpu.make_async_copy(rg_hbm, rin.at[1], rin_sem).start()
@@ -95,12 +97,12 @@
         t, col, wide = items[i]
         cols = pl.ds(col, wide)
         acc = jnp.zeros((8, wide), jnp.float32)
-        for h in range(2):
-            for copy in loads[2 * i + h]:
+        for _, h, deep, pair in [load for load in loads if load[0] == i]:
+            for copy in pair:
                 copy.wait()
 
-            def add(j, acc, h=h):
-                r = pl.ds(pl.multiple_of(h * half + j * STEP, STEP), STEP)
+            def add(j, acc, first=h * deep):
+                r = pl.ds(pl.multiple_of(first + j * STEP, STEP), STEP)
                 v = lat[t, r, cols] + oth[t, r, cols].astype(jnp.float32)
                 lat[t, r, cols] = v
                 v = v * v
@@ -108,7 +110,7 @@
                     acc = acc + v[8 * k : 8 * k + 8]
                 return acc
 
-            acc = lax.fori_loop(0, half // STEP, add, acc)
+            acc = lax.fori_loop(0, deep // STEP, add, acc)
         sums[t, x, :, cols] = jnp.sum(acc, axis=0, keepdims=True)
 
     def spread(piece, send, recv):
@@ -168,7 +170,7 @@
                     where = pl.ds(pl.multiple_of(x * rows + c * size + skip, STEP), size - skip)
                     piece = outs[t].at[0, where, cols]
                     for d, peer in enumerate((right, left)):
-                        recv = near_recv.at[d, t] if h == d else rest_recv.at[d]
+                        recv = near_recv.at[d, t] if h == d else rest_recv
                         remote(piece, piece, own_send, recv, peer).start()
 
     wait_bytes(raw, raw_recv)
@@ -195,13 +197,12 @@
     first.wait_recv()
     near = pl.ds(y * nc, nc)
     ups = remote(plane.at[near], plane.at[near], pl_send, pl_recv.at[1], y_up)
-    dns = remote(plane.at[near], plane.at[near], pl_send, pl_recv.at[2], y_dn)
+    dns = remote(plane.at[near], plane.at[near], pl_send, pl_recv.at[1], y_dn)
     ups.start()
     dns.start()
-    ups.wait_recv()
-    dns.wait_recv()
+    wait_bytes(plane.at[pl.ds(0, 2 * nc)], pl_recv.at[1])
     from_dn = pl.ds(step(y, -1, ny) * nc, nc)
-    far = remote(plane.at[from_dn], plane.at[from_dn], pl_send, pl_recv.at[3], y_up)
+    far = remote(plane.at[from_dn], plane.at[from_dn], pl_send, pl_recv.at[2], y_up)
     far.start()
     far.wait_recv()
     zring[z] = jnp.concatenate([plane[k] for k in range(ny * nc)], axis=0)
@@ -211,11 +212,10 @@
         moves = [remote(zring.at[at], zring.at[at], z_send, z_recv.at[s], z_up)]
         if s < hops_dn:
             at = step(z, s, nz)
-            moves.append(remote(zring.at[at], zring.at[at], z_send, z_recv.at[hops_up + s], z_dn))
+            moves.append(remote(zring.at[at], zring.at[at], z_send, z_recv.at[s], z_dn))
         for copy in moves:
             copy.start()
-        for copy in moves:
-            copy.wait_recv()
+        wait_bytes(zring.at[pl.ds(0, len(moves))], z_recv.at[s])
     for k in range(nz // 2):
         both = jnp.concatenate([zring[2 * k], zring[2 * k + 1]], axis=0)
         router[pl.ds(2 * k * ny * nc, 2 * ny * nc), :] = both.astype(jnp.bfloat16)
@@ -228,9 +228,7 @@
             where = pl.ds(pl.multiple_of(source * rows + d * half, half), half)
             piece = outs[t].at[0, where]
             remote(piece, piece, fwd_send, fwd_recv, (right, left)[d]).start()
-    for d in range(2):
-        count = 2 * half - (sent_raw if d == 1 else 0)
-        wait_bytes(out_g.at[0, pl.ds(0, count)], rest_recv.at[d])
+    wait_bytes(out_g.at[0, pl.ds(0, 4 * half - sent_raw)], rest_recv)
     wait_bytes(sums.at[:, pl.ds(0, nx - 1)], sum_send)
     wait_bytes(rx.at[pl.ds(0, nx - 1)], rx_send)
     wait_bytes(raw, raw_send)
@@ -285,9 +283,9 @@
             pltpu.VMEM((nx, 1, rows), jnp.float32),
             pltpu.VMEM((ny * nc, 1, whole), jnp.float32),
             pltpu.VMEM((nz, ny * nc, whole), jnp.float32),
-            dma((3, 2, 2)), dma(()), dma(()), dma((3,)), dma(()), dma(()), dma(()), dma(()),
-            dma(()), dma((2, 2)), dma((2,)), dma(()), dma(()),
-            dma(()), dma((4,)), dma(()), dma((nz - 1,)),
+            dma((4, 2)), dma(()), dma(()), dma((3,)), dma(()), dma(()), dma(()), dma(()),
+            dma(()), dma((2, 2)), dma(()), dma(()), dma(()),
+            dma(()), dma((3,)), dma(()), dma((nz // 2,)),
             pltpu.SemaphoreType.REGULAR,
         ],
         compiler_params=pltpu.CompilerParams(

time: 78.6 us -> 78.6 us (level)
  no operation moved by 1% of the time
where the time goes in v7:
time: 78.6 us; the launch traced here: 78.5 us
  Pallas kernels  77.8 us (99%)
    pallas_call x1, Pallas kernels, body(): pl.pallas_call(functools.partial(kernel, dims), out_shape=(pltpu.VMEM((1,...  74.4 us
    pallas_call x1, Pallas kernels, body(): pl.pallas_call(write_out, out_shape=tuple((pltpu.HBM(o.shape, o.dtype) fo...  3.42 us

profile of v7, /device:TPU:8, one launch (start us, length us, event | category | flops | bytes accessed | tf_op | source)
XLA Modules:
  0.0 78.5 jit_solution(5839846108889664041)
XLA Ops:
  0.6 74.4 %ring.1 = (bf16[1,2048,1024]{2,1,0:T(8,128)(2,1)S(1)}, bf16[1,2048,1024]{2,1,0:T(8,128)(2,1)S(1)}, f32[1,1024]{1,0:T(1,128)S(1)}, f32[1,1024]{1,0:T(1,128)S(1)}, bf16[64,2048]{1,0:T(8,128)(2,1)S(1)}) custom-call(f32[1,512,1024]{2,1,0:T(8,128)} %tg_hbm.1, bf16[1,512,1024]{2,1,0:T(8,128)(2,1)} %og_hbm.1, f32[1,512,1024]{2,1,0:T(8,128)} %tu_hbm.1, ...), custom_call_target="tpu_custom_call" | custom-call | tf_op jit(solution)/shard_map/ring/pallas_call | solution.py:266
  75.1 3.4 %write_out.1 = (bf16[1,2048,1024]{2,1,0:T(8,128)(2,1)}, bf16[1,2048,1024]{2,1,0:T(8,128)(2,1)}, f32[1,1024]{1,0:T(1,128)}, f32[1,1024]{1,0:T(1,128)}, bf16[64,2048]{1,0:T(8,128)(2,1)}) custom-call(bf16[1,2048,1024]{2,1,0:T(8,128)(2,1)S(1)} %get-tuple-element.15.refs_0_, bf16[1,2048,1024]{2,1,0:T(8,128)(2,1)S(1)} %get-tuple-element.16.refs_1_, ...), custom_call_target="tpu_custom_call" | custom-call | tf_op jit(solution)/shard_map/write_out/pallas_call | solution.py:296
